TPU v7x, 256 devices: a whole 4x4x8 slice. The times are simulated.
256 devices in a mesh: rows: 128 (over z, y_lo, x, core), dp: 2 (over y_hi).
Axes of the slice: x: 4, y: 4 (y_hi: 2, y_lo: 2; y = y_hi * 2 + y_lo), z: 8, core: 2. Of those that a mesh axis runs over, the one named last changes fastest.
Arguments:
- query_act: bfloat16 [1024, 512, 128], P(('dp', 'rows')), parts along dimension 0, may hold values from -2.09375 to 2.09375
- key_act: bfloat16 [1024, 512, 128], P(('dp', 'rows')), parts along dimension 0, may hold values from -2.09375 to 2.09375
- value_act: bfloat16 [1024, 512, 128], P(('dp', 'rows')), parts along dimension 0, may hold values from -4 to 4
- attn_out: bfloat16 [1024, 512, 128], P(('dp', 'rows')), parts along dimension 0, may hold values from -4 to 4
- grad_out: bfloat16 [1024, 512, 128], P(('dp', 'rows')), parts along dimension 0, may hold values from -24 to 24
- pair_bias: bfloat16 [4, 1024, 512], P(None, ('dp', 'rows')), parts along dimension 1, may hold values from -3 to 3
- log_norm: float32 [1024, 4, 512], P(('dp', 'rows')), parts along dimension 0, may hold values from 6.8 to 8
- back_weight: bfloat16 [384, 128], replicated, may hold values from -2 to 2
Outputs:
- column_grad: bfloat16 [512, 1024, 128], P('rows', 'dp'), parts along dimension 1
- bias_grad: float32 [4, 1024, 512], P(None, ('dp', 'rows')), parts along dimension 1
There are 2 independent parts, one for each index of `dp`. A program takes and returns all parts, laid end to end along the dimension named above; an argument that names none is the same for every part. Nothing has to cross between parts.
All inputs are finite; a program needn't handle non-finite values.
Results may differ from a plain program's by a relative error of at most 0.008.
Values may be sent and summed in bfloat16 or wider, within the bound.
No kernel may reach another device: no remote copies, remote signals or barrier semaphores. Data moves between devices by JAX's collectives and lax.ppermute only.
A program may use at most 64 MiB of HBM per device.

v0:
```python
import jax
import jax.numpy as jnp
from jax import lax
from jax.sharding import Mesh
from jax.sharding import PartitionSpec as P

ROWS = ("rows_0", "rows_1", "rows_2", "rows_3")
DP_ROWS = ("dp", "rows_0", "rows_1", "rows_2", "rows_3")


def split_up(x, dim, length):
    before, after = (x.shape[:dim], x.shape[dim + 1 :])
    return jnp.moveaxis(x.reshape(*before, length, -1, *after), dim, 0)


def summed_on_arrival(x, axis, dim):
    tiles = split_up(x, dim, lax.axis_size(axis))
    arrived = lax.all_to_all(tiles, axis, split_axis=0, concat_axis=0, tiled=True)
    return arrived.astype(jnp.float32).sum(axis=0)


def sum_by_axis(x, axes, dim):
    far, near = axes
    own = summed_on_arrival(split_up(x, dim, lax.axis_size(far)), near, dim + 1)
    return jnp.sum(
        lax.all_to_all(own.astype(jnp.bfloat16), far, 0, 0, tiled=True).astype(jnp.float32), axis=0
    )


def from_everyone(x, axis):
    copies = jnp.broadcast_to(x, (lax.axis_size(axis), *x.shape))
    return lax.all_to_all(copies, axis, split_axis=0, concat_axis=0, tiled=True)


def laid_out(tiles, dim):
    tiles = jnp.moveaxis(tiles, 0, dim)
    dims = tiles.shape
    return tiles.reshape(*dims[:dim], dims[dim] * dims[dim + 1], *dims[dim + 2 :])


def gather_axes(x, axes, dim):
    far, near = axes
    leading = from_everyone(x, far)
    tiles = jnp.swapaxes(from_everyone(leading, near), 0, 1)
    return laid_out(tiles.reshape(-1, *x.shape), dim)


def query_block(activations, bias_block, offset, row_span):
    query_act, key_act, value_act, attn_out, grad_out, log_norm = activations
    row_count, length, feature_width = query_act.shape
    head_count = bias_block.shape[0]
    head_size = feature_width // head_count
    softmax_scale = head_size ** (-0.5)
    query_part = lax.dynamic_slice_in_dim(query_act, offset, row_span, 1).reshape(
        row_count, row_span, head_count, head_size
    )
    grad_part = lax.dynamic_slice_in_dim(grad_out, offset, row_span, 1).reshape(
        row_count, row_span, head_count, head_size
    )
    out_part = lax.dynamic_slice_in_dim(attn_out, offset, row_span, 1).reshape(
        row_count, row_span, head_count, head_size
    )
    norm_part = lax.dynamic_slice_in_dim(log_norm, offset, row_span, 2)
    key_heads = key_act.reshape(row_count, length, head_count, head_size)
    value_heads = value_act.reshape(row_count, length, head_count, head_size)
    scores = (
        jnp.einsum("ijhd,ikhd->ihjk", query_part, key_heads, preferred_element_type=jnp.float32)
        * softmax_scale
        + bias_block.astype(jnp.float32)[None]
    )
    probs = jnp.exp(scores - norm_part[:, :, :, None])
    probs_low = probs.astype(jnp.bfloat16)
    grad_value = jnp.einsum(
        "ihjk,ijhd->ikhd", probs_low, grad_part, preferred_element_type=jnp.float32
    )
    grad_prob = jnp.einsum(
        "ijhd,ikhd->ihjk", grad_part, value_heads, preferred_element_type=jnp.float32
    )
    row_delta = jnp.einsum(
        "ijhd,ijhd->ihj", grad_part.astype(jnp.float32), out_part.astype(jnp.float32)
    )
    grad_score = probs * (grad_prob - row_delta[:, :, :, None])
    score_low = grad_score.astype(jnp.bfloat16)
    grad_query = (
        jnp.einsum("ihjk,ikhd->ijhd", score_low, key_heads, preferred_element_type=jnp.float32)
        * softmax_scale
    )
    grad_key = (
        jnp.einsum("ihjk,ijhd->ikhd", score_low, query_part, preferred_element_type=jnp.float32)
        * softmax_scale
    )
    return (jnp.sum(grad_score, axis=0), grad_query, grad_key, grad_value)


def run_blocks(activations, bias_rows, offset, row_span):
    query_act = activations[0]
    row_count, length, feature_width = query_act.shape
    head_count = bias_rows.shape[0]
    head_size = feature_width // head_count
    block_width = 1
    for candidate in range(min(row_span, 128), 0, -1):
        if row_span % candidate == 0:
            block_width = candidate
            break
    if block_width == row_span:
        return query_block(activations, bias_rows, offset, row_span)

    def advance(block_index, totals):
        bias_total, query_total, key_total, value_total = totals
        inner = block_index * block_width
        bias_block = lax.dynamic_slice_in_dim(bias_rows, inner, block_width, 1)
        partial_value, grad_query, grad_key, grad_value = query_block(
            activations, bias_block, offset + inner, block_width
        )
        bias_total = lax.dynamic_update_slice_in_dim(bias_total, partial_value, inner, 1)
        query_total = lax.dynamic_update_slice_in_dim(query_total, grad_query, inner, 1)
        return (bias_total, query_total, key_total + grad_key, value_total + grad_value)

    start_totals = (
        jnp.zeros((head_count, row_span, length), jnp.float32),
        jnp.zeros((row_count, row_span, head_count, head_size), jnp.float32),
        jnp.zeros((row_count, length, head_count, head_size), jnp.float32),
        jnp.zeros((row_count, length, head_count, head_size), jnp.float32),
    )
    return lax.fori_loop(0, row_span // block_width, advance, start_totals)


def reduce_bias(partial_value):
    return sum_by_axis(
        partial_value.astype(jnp.bfloat16), (("rows_0", "rows_1", "rows_2"), "rows_3"), 1
    )


def local(query_act, key_act, value_act, attn_out, grad_out, pair_bias, log_norm, back_weight):
    row_count, length, feature_width = query_act.shape
    activations = (query_act, key_act, value_act, attn_out, grad_out, log_norm)
    bias_full = gather_axes(pair_bias, (("rows_0", "rows_1", "rows_2"), "rows_3"), 1)
    partial_value, grad_query, grad_key, grad_value = run_blocks(activations, bias_full, 0, length)
    bias_grad = reduce_bias(partial_value)
    joined = jnp.concatenate(
        [
            grad_query.reshape(row_count, length, feature_width),
            grad_key.reshape(row_count, length, feature_width),
            grad_value.reshape(row_count, length, feature_width),
        ],
        axis=2,
    ).astype(jnp.bfloat16)
    pair_rows = jnp.dot(joined, back_weight, preferred_element_type=jnp.float32).astype(
        jnp.bfloat16
    )
    swapped = jnp.transpose(pair_rows, (1, 0, 2))
    column_grad = lax.all_to_all(swapped, ROWS, split_axis=0, concat_axis=1, tiled=True)
    return (column_grad, bias_grad)


def solution(mesh):
    finer = Mesh(
        mesh.devices.reshape(8, 2, 4, 2, mesh.shape["dp"]),
        ("rows_0", "rows_1", "rows_2", "rows_3", "dp"),
    )
    return jax.shard_map(
        local,
        mesh=finer,
        in_specs=(
            P(DP_ROWS, None, None),
            P(DP_ROWS, None, None),
            P(DP_ROWS, None, None),
            P(DP_ROWS, None, None),
            P(DP_ROWS, None, None),
            P(None, DP_ROWS, None),
            P(DP_ROWS, None, None),
            P(),
        ),
        out_specs=(P(ROWS, "dp", None), P(None, DP_ROWS, None)),
        check_vma=False,
    )
```

profile of v0, /device:TPU:2, one launch (start us, length us, event | category | flops | bytes accessed | tf_op | source)
XLA Modules:
  0.0 191.8 jit_solution(2115380036355374354)
XLA Ops:
  0.7 2.3 %broadcast_in_dim.19 = bf16[64,4,4,512]{3,2,1,0:T(4,128)(2,1)} broadcast(bf16[4,4,512]{2,1,0:T(4,128)(2,1)} %param.15), dimensions={1,2,3} | broadcast | bytes 1064960 | tf_op jit(solution)/shard_map/broadcast_in_dim | solution.py:31
  3.0 13.2 %all-to-all-start = ((bf16[64,4,4,512]{3,2,1,0:T(4,128)(2,1)}), bf16[64,4,4,512]{3,2,1,0:T(4,128)(2,1)}, u32[]{:S(2)}, u32[]{:S(2)}) async-start(bf16[64,4,4,512]{3,2,1,0:T(4,128)(2,1)} %broadcast_in_dim.19), calls=%async_computation | async-start | bytes 2097152 | tf_op jit(solution)/shard_map/all_to_all | solution.py:32
  16.4 1.2 copy.77
  17.7 26.3 %all-to-all-done = bf16[64,4,4,512]{3,2,1,0:T(4,128)(2,1)} async-done(((bf16[64,4,4,512]{3,2,1,0:T(4,128)(2,1)}), bf16[64,4,4,512]{3,2,1,0:T(4,128)(2,1)}, u32[]{:S(2)}, u32[]{:S(2)}) %all-to-all-start) | async-done | bytes 1048608 | tf_op jit(solution)/shard_map/all_to_all | solution.py:32
  44.0 1.6 copy.70
  46.2 5.4 %all_to_all.38 = bf16[2,64,4,4,512]{4,3,1,2,0:T(4,128)(2,1)S(1)} all-to-all(bf16[2,64,4,4,512]{4,3,1,2,0:T(4,128)(2,1)S(1)} %broadcast_in_dim.20), channel_id=1, replica_groups=mesh['rows_0'=8,'rows_1'=2,'rows_2'=4,'rows_3'=2,'dp'=2] {'rows_3'}, dimensions={0} | all-to-all | bytes 4194304 | tf_op jit(solution)/shard_map/all_to_all | solution.py:32
  51.6 1.2 copy.71
  52.8 2.5 %copy.72 = bf16[4,128,4,512]{3,0,2,1:T(4,128)(2,1)} copy(bf16[4,128,4,512]{3,2,0,1:T(4,128)(2,1)S(1)} %bitcast.103) | data formatting | bytes 4194304 | tf_op jit(solution)/shard_map/transpose | solution.py:36
  56.1 1.5 broadcast_in_dim.18
  57.6 55.6 %while.20 = (s32[]{:T(128)}, bf16[4,512,512]{2,1,0:T(8,128)(2,1)}, bf16[4,512,4,32]{1,3,2,0:T(8,128)(2,1)}, f32[4,512,4,32]{1,3,2,0:T(8,128)S(1)}, f32[4,512,4,3...) while((s32[]{:T(128)}, bf16[4,512,512]{2,1,0:T(8,128)(2,1)}, ...), condition=%wide.region_2.0_spmd.clone, body=%wide.region_0.0_spmd.clone.sunk | while | flops 348715008 | bytes 37798180 | solution.py:125
  59.4 1.6 constant_dynamic-slice_fusion.9
  61.8 1.0 copy.107
  62.8 1.0 fusion.68
  63.8 1.2 constant_dynamic-slice_fusion.11
  65.9 1.3 fusion.73
  67.3 1.8 fusion.70
  73.3 1.6 constant_dynamic-slice_fusion.9
  75.7 1.0 copy.107
  77.7 1.2 constant_dynamic-slice_fusion.11
  79.8 1.3 fusion.73
  81.1 1.8 fusion.70
  87.2 1.6 constant_dynamic-slice_fusion.9
  89.6 1.0 copy.107
  90.6 1.0 fusion.68
  91.6 1.2 constant_dynamic-slice_fusion.11
  93.7 1.3 fusion.73
  95.0 1.8 fusion.70
  101.1 1.6 constant_dynamic-slice_fusion.9
  103.5 1.0 copy.107
  105.5 1.2 constant_dynamic-slice_fusion.11
  107.6 1.3 fusion.73
  108.9 1.8 fusion.70
  113.3 1.0 copy.81
  114.3 2.3 %copy.84 = bf16[64,4,8,512]{3,0,2,1:T(8,128)(2,1)S(1)} copy(bf16[64,4,8,512]{3,2,0,1:T(8,128)(2,1)} %bitcast.101) | data formatting | bytes 4194304 | tf_op jit(solution)/shard_map/transpose | solution.py:13
  116.6 3.0 %copy.85 = bf16[2,64,4,4,512]{4,3,1,2,0:T(4,128)(2,1)} copy(bf16[2,64,4,4,512]{4,1,3,0,2:T(8,128)(2,1)S(1)} %bitcast.104) | data formatting | bytes 4194304 | tf_op jit(solution)/shard_map/transpose | solution.py:13
  119.6 3.9 %all-to-all-start.3 = ((bf16[2,64,4,4,512]{4,3,1,2,0:T(4,128)(2,1)}), bf16[2,64,4,4,512]{4,3,1,2,0:T(4,128)(2,1)S(1)}, u32[]{:S(2)}, u32[]{:S(2)}) async-start(bf16[2,64,4,4,512]{4,3,1,2,0:T(4,128)(2,1)} %copy.85), calls=%async_computation.3 | async-start | bytes 4194304 | tf_op jit(solution)/shard_map/all_to_all | solution.py:18
  123.5 2.1 %copy.79 = bf16[4,512,128]{2,1,0:T(8,128)(2,1)} copy(bf16[4,512,128]{1,2,0:T(8,128)(2,1)} %bitcast.107) | data formatting | bytes 1048576 | tf_op jit(solution)/shard_map/reshape | solution.py:142
  126.4 1.3 copy.80
  127.8 1.8 fusion.26
  129.5 1.2 copy.82
  130.7 8.1 %all-to-all-start.2 = ((bf16[512,4,128]{2,1,0:T(4,128)(2,1)}), bf16[512,4,128]{2,1,0:T(4,128)(2,1)}, u32[]{:S(2)}, u32[]{:S(2)}) async-start(bf16[512,4,128]{2,1,0:T(4,128)(2,1)} %copy.82), calls=%async_computation.2 | async-start | bytes 1048576 | tf_op jit(solution)/shard_map/all_to_all | solution.py:152
  138.8 2.4 %reduce_sum.34 = bf16[64,4,4,512]{3,2,0,1:T(4,128)(2,1)S(1)} reduce(bf16[2,64,4,4,512]{4,3,1,2,0:T(4,128)(2,1)S(1)} %all-to-all-done.3, bf16[]{:T(256)} %constant.49.clone.1), dimensions={0}, to_apply=%region_3.0 | reduce | flops 524288 | bytes 3145730 | tf_op jit(solution)/shard_map/reduce_sum | solution.py:19
  141.2 1.6 copy.87
  142.8 14.4 %all-to-all-done.2 = bf16[512,4,128]{2,1,0:T(4,128)(2,1)} async-done(((bf16[512,4,128]{2,1,0:T(4,128)(2,1)}), bf16[512,4,128]{2,1,0:T(4,128)(2,1)}, u32[]{:S(2)}, u32[]{:S(2)}) %all-to-all-start.2) | async-done | bytes 524320 | tf_op jit(solution)/shard_map/all_to_all | solution.py:152
  157.2 5.5 %all-to-all-start.4 = ((bf16[64,4,4,512]{3,2,1,0:T(4,128)(2,1)}), bf16[64,4,4,512]{3,2,1,0:T(4,128)(2,1)S(1)}, u32[]{:S(2)}, u32[]{:S(2)}) async-start(bf16[64,4,4,512]{3,2,1,0:T(4,128)(2,1)} %copy.87), calls=%async_computation.4 | async-start | bytes 2097152 | tf_op jit(solution)/shard_map/all_to_all | solution.py:26
  162.7 2.0 %copy.83 = bf16[4,128,4,128]{3,2,1,0:T(4,128)(2,1)} copy(bf16[4,128,4,128]{3,2,0,1:T(4,128)(2,1)} %bitcast.12) | data formatting | bytes 1048576 | tf_op jit(solution)/shard_map/all_to_all | solution.py:152
  164.7 26.0 %all-to-all-done.4 = bf16[64,4,4,512]{3,2,1,0:T(4,128)(2,1)S(1)} async-done(((bf16[64,4,4,512]{3,2,1,0:T(4,128)(2,1)}), bf16[64,4,4,512]{3,2,1,0:T(4,128)(2,1)S(1)}, u32[]{:S(2)}, u32[]{:S(2)}) %all-to-all-start.4) | async-done | bytes 1048608 | tf_op jit(solution)/shard_map/all_to_all | solution.py:26
  190.7 1.1 convert_reduce_fusion
  (66 shorter events, 27.9 us)
Async XLA Ops:
  0.6 127.1 %copy-start = (bf16[384,128]{1,0:T(8,128)(2,1)S(1)}, bf16[384,128]{1,0:T(8,128)(2,1)}, u32[]{:S(2)}) copy-start(bf16[384,128]{1,0:T(8,128)(2,1)} %param.17) | copy-start | bytes 294916
  0.6 15.6 %copy-start.3 = (bf16[4,512,128]{2,1,0:T(8,128)(2,1)S(1)}, bf16[4,512,128]{2,1,0:T(8,128)(2,1)}, u32[]{:S(2)}) copy-start(bf16[4,512,128]{2,1,0:T(8,128)(2,1)} %param.11) | copy-start | bytes 1572868
  3.0 41.1 %all-to-all-start = ((bf16[64,4,4,512]{3,2,1,0:T(4,128)(2,1)}), bf16[64,4,4,512]{3,2,1,0:T(4,128)(2,1)}, u32[]{:S(2)}, u32[]{:S(2)}) async-start(bf16[64,4,4,512]{3,2,1,0:T(4,128)(2,1)} %broadcast_in_dim.19), calls=%async_computation | async-start | bytes 2097152 | tf_op jit(solution)/shard_map/all_to_all | solution.py:32
  67.2 1.8 copy-start.1
  69.9 0.8 copy-start.2
  81.1 1.8 copy-start.1
  83.8 0.8 copy-start.2
  95.0 1.8 copy-start.1
  97.7 0.8 copy-start.2
  108.9 1.8 copy-start.1
  111.6 0.8 copy-start.2
  119.6 11.2 %all-to-all-start.3 = ((bf16[2,64,4,4,512]{4,3,1,2,0:T(4,128)(2,1)}), bf16[2,64,4,4,512]{4,3,1,2,0:T(4,128)(2,1)S(1)}, u32[]{:S(2)}, u32[]{:S(2)}) async-start(bf16[2,64,4,4,512]{4,3,1,2,0:T(4,128)(2,1)} %copy.85), calls=%async_computation.3 | async-start | bytes 4194304 | tf_op jit(solution)/shard_map/all_to_all | solution.py:18
  130.7 26.4 %all-to-all-start.2 = ((bf16[512,4,128]{2,1,0:T(4,128)(2,1)}), bf16[512,4,128]{2,1,0:T(4,128)(2,1)}, u32[]{:S(2)}, u32[]{:S(2)}) async-start(bf16[512,4,128]{2,1,0:T(4,128)(2,1)} %copy.82), calls=%async_computation.2 | async-start | bytes 1048576 | tf_op jit(solution)/shard_map/all_to_all | solution.py:152
  157.2 33.5 %all-to-all-start.4 = ((bf16[64,4,4,512]{3,2,1,0:T(4,128)(2,1)}), bf16[64,4,4,512]{3,2,1,0:T(4,128)(2,1)S(1)}, u32[]{:S(2)}, u32[]{:S(2)}) async-start(bf16[64,4,4,512]{3,2,1,0:T(4,128)(2,1)} %copy.87), calls=%async_computation.4 | async-start | bytes 2097152 | tf_op jit(solution)/shard_map/all_to_all | solution.py:26
where the time goes:
time: 193 us; the launch traced here: 192 us
  waiting for transfers between devices  66.7 us (35%)
  local copies, waits for them, and re-layouts  56.5 us (29%)
  starting transfers between devices  30.8 us (16%)
  matrix products  22.5 us (12%)
  other arithmetic  8.8 us (5%)
  blocking collectives  5.42 us (3%)
    all_to_all x1, waiting for transfers between devices, from_everyone(): return lax.all_to_all(copies, axis, split_axis=0, concat_axis=0, tiled=True)  26.3 us
    all_to_all x1, waiting for transfers between devices, sum_by_axis(): lax.all_to_all(own.astype(jnp.bfloat16), far, 0, 0, tiled=True)  26 us
    all_to_all x1, waiting for transfers between devices, local(): lax.all_to_all(swapped, ROWS, split_axis=0, concat_axis=1, tiled=True)  14.4 us
    all_to_all x1, starting transfers between devices, from_everyone(): return lax.all_to_all(copies, axis, split_axis=0, concat_axis=0, tiled=True)  13.2 us
    dynamic_slice x8, local copies, waits for them, and re-layouts, query_block(): lax.dynamic_slice_in_dim(attn_out, offset, row_span, 1)  9.66 us
    all_to_all x1, starting transfers between devices, local(): lax.all_to_all(swapped, ROWS, split_axis=0, concat_axis=1, tiled=True)  8.1 us
    dot_general x4, matrix products, query_block(): jnp.einsum('ijhd,ikhd->ihjk', grad_part, value_heads, preferred_element_t...  7.16 us
    all_to_all x1, starting transfers between devices, sum_by_axis(): lax.all_to_all(own.astype(jnp.bfloat16), far, 0, 0, tiled=True)  5.51 us
  transfers between devices with their start and end apart: 4, of which 3 were waited for; matrix products, arithmetic and copies ran while one was open for 8% of the time, Pallas kernels for 0%

commit v1 on v0

v1 whole, which is shorter than its diff:
```python
import functools

import jax
import jax.numpy as jnp
from jax import lax
from jax.experimental import pallas as pl
from jax.experimental.pallas import tpu as pltpu
from jax.sharding import Mesh
from jax.sharding import PartitionSpec as P

Z, Y, X, C = ("rows_0", "rows_1", "rows_2", "rows_3")
ROWS = (Z, Y, X, C)
DP_ROWS = ("dp",) + ROWS
PLANE = (Y, X)
LINE = (Z, C)
LOG2E = 1.4426950408889634


def exchange(x, axes):
    return lax.all_to_all(x, axes, split_axis=0, concat_axis=0, tiled=True)


def across(x):
    return lax.ppermute(x, C, [(0, 1), (1, 0)])


def attention_rows(
    first, core_ref, q_ref, k_ref, v_ref, o_ref, g_ref, ln_ref, bias_ref, w_ref, *rest
):
    if first:
        pair_ref, db_ref, b2, kvt, qt, gt = rest
    else:
        before_ref, pair_ref, wire_ref, b2, kvt, qt, gt, db_ref = rest
    step = pl.program_id(0)
    planes, heads, lines, tall, length = bias_ref.shape
    width = q_ref.shape[2]
    size = 32
    scale = size**-0.5
    core = core_ref[0]

    @pl.when(step == 0)
    def _():
        for h in range(heads):
            for a in range(planes):
                for z in range(lines):
                    at = (z * planes + a) * tall
                    b2[h, at : at + tall, :] = bias_ref[a, h, z].astype(jnp.float32) * LOG2E
        if first:
            db_ref[...] = jnp.zeros_like(db_ref)
        else:
            db_ref[...] = before_ref[...]

    q, k, v, g = q_ref[0], k_ref[0], v_ref[0], g_ref[0]
    qt[...] = q.T
    gt[...] = g.T
    kt = k.T
    vt = v.T
    product = g.astype(jnp.float32) * o_ref[0].astype(jnp.float32)
    lane = lax.broadcasted_iota(jnp.int32, (1, width), 1)
    ln_lane = lax.broadcasted_iota(jnp.int32, (1, ln_ref.shape[2]), 1)
    block = 256
    grad_q = [None] * (length // block)
    for h in range(heads):
        head = core * heads + h
        mine = (lane // size) == head
        ln = jnp.sum(jnp.where(ln_lane == head, ln_ref[0], 0.0), axis=1, keepdims=True) * LOG2E
        delta = jnp.sum(jnp.where(mine, product, 0.0), axis=1, keepdims=True)
        zero = jnp.zeros_like(q)
        qh = jnp.where(mine, q, zero)
        gh = jnp.where(mine, g, zero)
        kh = jnp.where(mine, k, zero)
        rows = pl.ds(pl.multiple_of(head * size, size), size)
        qth = qt[rows, :]
        gth = gt[rows, :]
        grad_k = None
        for b in range(length // block):
            span = slice(b * block, (b + 1) * block)
            s = jnp.dot(qh[span], kt, preferred_element_type=jnp.float32)
            d = jnp.dot(gh[span], vt, preferred_element_type=jnp.float32)
            p = jnp.exp2(s * (scale * LOG2E) + b2[h, span, :] - ln[span])
            ds = p * (d - delta[span])
            db_ref[h, span, :] += ds
            pb = p.astype(jnp.bfloat16)
            dsb = ds.astype(jnp.bfloat16)
            gv = jnp.dot(gth[:, span], pb, preferred_element_type=jnp.float32)
            gk = jnp.dot(qth[:, span], dsb, preferred_element_type=jnp.float32)
            gq = jnp.dot(dsb, kh, preferred_element_type=jnp.float32)
            grad_k = gk if grad_k is None else grad_k + gk
            grad_v = gv if b == 0 else grad_v + gv
            grad_q[b] = gq if grad_q[b] is None else grad_q[b] + gq
        kvt[h * size : (h + 1) * size, :] = (grad_k * scale).astype(jnp.bfloat16)
        kvt[(heads + h) * size : (heads + h + 1) * size, :] = grad_v.astype(jnp.bfloat16)
    half = heads * size
    own = pl.multiple_of(core * half, half)
    w_kv = jnp.concatenate(
        [w_ref[pl.ds(width + own, half), :], w_ref[pl.ds(2 * width + own, half), :]], axis=0
    )
    kv = kvt[...].T
    for b in range(length // block):
        span = slice(b * block, (b + 1) * block)
        total = jnp.dot(
            (grad_q[b] * scale).astype(jnp.bfloat16), w_ref[:width, :], preferred_element_type=jnp.float32
        ) + jnp.dot(kv[span], w_kv, preferred_element_type=jnp.float32)
        pair_ref[0, span, :] = total.astype(pair_ref.dtype)

    if not first:

        @pl.when(step == pl.num_programs(0) - 1)
        def _():
            for h in range(heads):
                for a in range(planes):
                    for z in range(lines):
                        at = (z * planes + a) * tall
                        wire_ref[a, h, z] = db_ref[h, at : at + tall, :].astype(wire_ref.dtype)


def run_rows(core, acts, bias, weight, before=None):
    first = before is None
    rows, length, width = acts[0].shape
    heads = bias.shape[1]
    row = pl.BlockSpec((1, length, width), lambda i: (i, 0, 0))
    whole = lambda x: pl.BlockSpec(x.shape, lambda i: (0,) * len(x.shape))
    ln = acts[-1]
    in_specs = [pl.BlockSpec(memory_space=pltpu.SMEM)] + [row] * 5
    in_specs += [pl.BlockSpec((1,) + ln.shape[1:], lambda i: (i, 0, 0)), whole(bias), whole(weight)]
    args = [core, *acts, bias, weight]
    square = jax.ShapeDtypeStruct((heads, length, length), jnp.float32)
    scratch = [
        pltpu.VMEM(square.shape, jnp.float32),
        pltpu.VMEM((width, length), jnp.bfloat16),
        pltpu.VMEM((width, length), jnp.bfloat16),
        pltpu.VMEM((width, length), jnp.bfloat16),
    ]
    if first:
        outs = [jax.ShapeDtypeStruct((rows, length, width), jnp.bfloat16), square]
        out_specs = [row, whole(square)]
    else:
        args.append(before)
        in_specs.append(whole(before))
        outs = [
            jax.ShapeDtypeStruct((rows, length, width), jnp.float32),
            jax.ShapeDtypeStruct(bias.shape, jnp.bfloat16),
        ]
        out_specs = [row, whole(bias)]
        scratch.append(pltpu.VMEM(square.shape, jnp.float32))
    return pl.pallas_call(
        functools.partial(attention_rows, first),
        grid=(rows,),
        in_specs=in_specs,
        out_specs=out_specs,
        out_shape=outs,
        scratch_shapes=scratch,
        compiler_params=pltpu.CompilerParams(dimension_semantics=("arbitrary",)),
        cost_estimate=pl.CostEstimate(
            flops=10 * rows * heads * length * length * width,
            bytes_accessed=8 * 1024 * 1024,
            transcendentals=rows * heads * length * length,
        ),
        name="partner_rows" if first else "own_rows",
    )(*args)


def local(query_act, key_act, value_act, attn_out, grad_out, pair_bias, log_norm, back_weight):
    heads, tall, length = pair_bias.shape
    z_n, c_n = lax.axis_size(Z), lax.axis_size(C)
    p_n = lax.axis_size(Y) * lax.axis_size(X)
    near = heads // c_n
    core = lax.axis_index(C).astype(jnp.int32).reshape(1)

    tiles = jnp.broadcast_to(
        pair_bias.reshape(1, c_n, near * tall, length), (z_n, c_n, near * tall, length)
    )
    lines = exchange(tiles.reshape(z_n * c_n, near * tall, length), LINE)
    lines = lines.reshape(z_n, c_n, near, tall, length).transpose(2, 0, 1, 3, 4)
    lines = lines.reshape(1, near * z_n * c_n * tall, length)
    planes = exchange(jnp.broadcast_to(lines, (p_n, *lines.shape[1:])), PLANE)
    bias = planes.reshape(p_n, near, z_n, c_n * tall, length)

    own = (query_act, key_act, value_act, attn_out, grad_out, jnp.swapaxes(log_norm, 1, 2))
    other = tuple(across(x) for x in own[:5]) + (jnp.swapaxes(across(log_norm), 1, 2),)

    sent, half_sum = run_rows(core, other, bias, back_weight)
    kept, terms = run_rows(core, own, bias, back_weight, half_sum)
    pair_rows = (kept + across(sent).astype(jnp.float32)).astype(jnp.bfloat16)

    summed = exchange(terms.reshape(p_n, -1, length), PLANE).astype(jnp.float32).sum(axis=0)
    summed = summed.reshape(near, z_n, c_n, tall, length).transpose(1, 2, 0, 3, 4)
    summed = summed.astype(jnp.bfloat16).reshape(z_n * c_n, near * tall, length)
    summed = exchange(summed, LINE).reshape(z_n, heads, tall, length)
    bias_grad = summed.astype(jnp.float32).sum(axis=0)

    swapped = jnp.transpose(pair_rows, (1, 0, 2))
    column_grad = lax.all_to_all(swapped, ROWS, split_axis=0, concat_axis=1, tiled=True)
    return (column_grad, bias_grad)


def solution(mesh):
    finer = Mesh(mesh.devices.reshape(8, 2, 4, 2, mesh.shape["dp"]), (*ROWS, "dp"))
    row = P(DP_ROWS, None, None)
    return jax.shard_map(
        local,
        mesh=finer,
        in_specs=(row, row, row, row, row, P(None, DP_ROWS, None), row, P()),
        out_specs=(P(ROWS, "dp", None), P(None, DP_ROWS, None)),
        check_vma=False,
    )
```

time: 193 us -> 125 us (0.65)
  local copies, waits for them, and re-layouts: 56.5 us -> 8.69 us
  Pallas kernels: 0 us -> 22.7 us
  matrix products: 22.5 us -> 0 us
  waiting for transfers between devices: 66.7 us -> 51.2 us
  blocking collectives: 5.42 us -> 17 us
  starting transfers between devices: 30.8 us -> 21.9 us
  other arithmetic: 8.8 us -> 0.92 us
    dynamic_slice x28 -> x0, local copies, waits for them, and re-layouts: 25.6 us -> none  [the longest x8 9.66 us: query_block(): lax.dynamic_slice_in_dim(attn_out, offset, row_span, 1)]
    pallas_call x0 -> x2, Pallas kernels: none -> 22.7 us  [run_rows(): pl.pallas_call(functools.partial(attention_rows, first), grid=(rows,), in...]
    dot_general x21 -> x0, matrix products: 22.5 us -> none  [the longest x4 7.16 us: query_block(): jnp.einsum('ijhd,ikhd->ihjk', grad_part, value_heads, preferred_element_t...]
    all_to_all x3, waiting for transfers between devices: 52.3 us -> 32.2 us  [exchange(): return lax.all_to_all(x, axes, split_axis=0, concat_axis=0, tiled=True)]
    all_to_all x1, blocking collectives: 5.42 us -> 17 us  [exchange(): return lax.all_to_all(x, axes, split_axis=0, concat_axis=0, tiled=True)]
    all_to_all x3, starting transfers between devices: 22.7 us -> 14.1 us  [exchange(): return lax.all_to_all(x, axes, split_axis=0, concat_axis=0, tiled=True)]
    transpose x4 -> x2, local copies, waits for them, and re-layouts: 8.98 us -> 1.25 us  [the longest x1 1.2 us: local(): swapped = jnp.transpose(pair_rows, (1, 0, 2))]
    dot_general x4 -> x0, other arithmetic: 3.85 us -> none  [query_block(): jnp.einsum('ijhd,ijhd->ihj', grad_part.astype(jnp.float32), out_part.asty...]
  transfers between devices with their start and end apart: 4 -> 11, of which waited for: 3 -> 7; matrix products, arithmetic and copies ran while one was open for 8% -> 5% of each run, Pallas kernels for 0% -> 0%
where the time goes in v1:
time: 125 us; the launch traced here: 123 us
  waiting for transfers between devices  51.2 us (41%)
  Pallas kernels  22.7 us (18%)
  starting transfers between devices  21.9 us (18%)
  blocking collectives  17 us (14%)
  local copies, waits for them, and re-layouts  8.69 us (7%)
    all_to_all x3, waiting for transfers between devices, exchange(): return lax.all_to_all(x, axes, split_axis=0, concat_axis=0, tiled=True)  32.2 us
    pallas_call x2, Pallas kernels, run_rows(): pl.pallas_call(functools.partial(attention_rows, first), grid=(rows,), in...  22.7 us
    all_to_all x1, waiting for transfers between devices, local(): lax.all_to_all(swapped, ROWS, split_axis=0, concat_axis=1, tiled=True)  18 us
    all_to_all x1, blocking collectives, exchange(): return lax.all_to_all(x, axes, split_axis=0, concat_axis=0, tiled=True)  17 us
    all_to_all x3, starting transfers between devices, exchange(): return lax.all_to_all(x, axes, split_axis=0, concat_axis=0, tiled=True)  14.1 us
    all_to_all x1, starting transfers between devices, local(): lax.all_to_all(swapped, ROWS, split_axis=0, concat_axis=1, tiled=True)  6.36 us
  transfers between devices with their start and end apart: 11, of which 7 were waited for; matrix products, arithmetic and copies ran while one was open for 5% of the time, Pallas kernels for 0%

profile of v1, /device:TPU:2, one launch (start us, length us, event | category | flops | bytes accessed | tf_op | source)
XLA Modules:
  0.0 123.3 jit_solution(8499630084591627300)
XLA Ops:
  0.6 0.7 broadcast_in_dim.14
  1.4 17.0 %all_to_all.38 = bf16[16,8,512]{2,1,0:T(8,128)(2,1)S(1)} all-to-all(bf16[16,8,512]{2,1,0:T(8,128)(2,1)S(1)} %bitcast.21), channel_id=1, replica_groups=mesh['rows_0'=8,'rows_1'=2,'rows_2'=4,'rows_3'=2,'dp'=2] {'rows_0','rows..., dimensions={0} | all-to-all | bytes 262144 | tf_op jit(solution)/shard_map/all_to_all | solution.py:20
  18.4 0.0 copy-start.2
  18.4 0.0 copy-start.6
  18.5 1.1 broadcast_in_dim.17
  19.6 5.8 %all-to-all-start.1 = ((bf16[8,128,512]{2,1,0:T(8,128)(2,1)}), bf16[8,128,512]{2,1,0:T(8,128)(2,1)S(1)}, u32[]{:S(2)}, u32[]{:S(2)}) async-start(bf16[8,128,512]{2,1,0:T(8,128)(2,1)} %broadcast_in_dim.17), calls=%async_computation.1 | async-start | bytes 2097152 | tf_op jit(solution)/shard_map/all_to_all | solution.py:20
  25.5 0.0 copy-done.2
  25.5 0.1 collective-permute-start.5
  25.6 0.0 copy-done.3
  25.6 0.4 collective-permute-start
  26.0 0.0 copy-done.4
  26.0 0.1 collective-permute-start.1
  26.1 0.0 copy-done.5
  26.1 0.4 collective-permute-start.2
  26.5 0.0 copy-done.6
  26.5 0.1 collective-permute-start.3
  26.6 0.1 collective-permute-done.5
  26.7 0.3 collective-permute-start.4
  27.0 1.3 %copy.21 = f32[4,4,512]{1,2,0:T(8,128)} copy(f32[4,4,512]{2,1,0:T(4,128)S(1)} %copy-done.2) | data formatting | bytes 65536 | tf_op args[6]
  28.4 1.3 %copy.23 = f32[4,4,512]{1,2,0:T(8,128)} copy(f32[4,4,512]{2,1,0:T(4,128)S(1)} %collective-permute-done.5) | data formatting | bytes 65536 | tf_op jit(solution)/shard_map/ppermute | solution.py:24
  29.7 0.0 collective-permute-done.q_ref
  29.7 0.0 collective-permute-done.1.k_ref
  29.7 0.0 collective-permute-done.2.v_ref
  29.7 0.2 collective-permute-done.3.o_ref
  29.9 0.7 collective-permute-done.4.g_ref
  30.7 10.2 %all-to-all-done.1 = bf16[8,128,512]{2,1,0:T(8,128)(2,1)S(1)} async-done(((bf16[8,128,512]{2,1,0:T(8,128)(2,1)}), bf16[8,128,512]{2,1,0:T(8,128)(2,1)S(1)}, u32[]{:S(2)}, u32[]{:S(2)}) %all-to-all-start.1) | async-done | bytes 1048608 | tf_op jit(solution)/shard_map/all_to_all | solution.py:20
  40.8 1.0 copy-done
  41.8 10.8 %partner_rows.1 = (bf16[4,512,128]{2,1,0:T(8,128)(2,1)}, f32[2,512,512]{2,1,0:T(8,128)}) custom-call(s32[1]{0:T(128)} %bitcast.core_ref, bf16[4,512,128]{2,1,0:T(8,128)(2,1)} %collective-permute-done.q_ref, bf16[4,512,128]{2,1,0:T(8,128)(2,1)} %collective-permute-done.1.k_ref, bf16[4,512,128]{2,1,0:T(8,128)(2,1)} %collective-permute-done.2.v_ref, ...), custom_call_target="tpu_custom_call" | custom-call | flops 2684354560 | bytes 8388608 | tf_op jit(solution)/shard_map/partner_rows/pallas_call | solution.py:146
  52.6 11.9 %own_rows.1 = (f32[4,512,128]{2,1,0:T(8,128)}, bf16[8,2,8,8,512]{4,3,2,1,0:T(8,128)(2,1)}) custom-call(s32[1]{0:T(128)} %bitcast.core_ref, bf16[4,512,128]{2,1,0:T(8,128)(2,1)} %q_ref.1, bf16[4,512,128]{2,1,0:T(8,128)(2,1)} %k_ref.1, bf16[4,512,128]{2,1,0:T(8,128)(2,1)} %v_ref.1, bf16[4,512,128]{2,1,0:T(8,128)(2,1)} %o_ref.1, bf16[4,512,128]{2,1,0:T(8,128)(2,1)} %g_ref.1, ...), custom_call_target="tpu_custom_call" | custom-call | flops 2684354560 | bytes 8388608 | tf_op jit(solution)/shard_map/own_rows/pallas_call | solution.py:146
  64.5 0.0 copy-start.7
  64.5 0.0 copy-start.1
  64.5 4.8 %all-to-all-start.3 = ((bf16[8,128,512]{2,1,0:T(8,128)(2,1)}), bf16[8,128,512]{2,1,0:T(8,128)(2,1)S(1)}, u32[]{:S(2)}, u32[]{:S(2)}) async-start(bf16[8,128,512]{2,1,0:T(8,128)(2,1)} %bitcast.19), calls=%async_computation.3 | async-start | bytes 2097152 | tf_op jit(solution)/shard_map/all_to_all | solution.py:20
  69.3 0.0 copy-done.7
  69.3 0.0 collective-permute-start.6
  69.3 14.7 %all-to-all-done.3 = bf16[8,128,512]{2,1,0:T(8,128)(2,1)S(1)} async-done(((bf16[8,128,512]{2,1,0:T(8,128)(2,1)}), bf16[8,128,512]{2,1,0:T(8,128)(2,1)S(1)}, u32[]{:S(2)}, u32[]{:S(2)}) %all-to-all-start.3) | async-done | bytes 1048608 | tf_op jit(solution)/shard_map/all_to_all | solution.py:20
  84.0 0.1 reduce_sum.21
  84.3 0.7 reshape.36
  85.0 3.5 %all-to-all-start.4 = ((bf16[16,8,512]{2,1,0:T(8,128)(2,1)}), bf16[16,8,512]{2,1,0:T(8,128)(2,1)S(1)}, u32[]{:S(2)}, u32[]{:S(2)}) async-start(bf16[16,8,512]{2,1,0:T(8,128)(2,1)} %reshape.36), calls=%async_computation.4 | async-start | bytes 262144 | tf_op jit(solution)/shard_map/all_to_all | solution.py:20
  88.5 0.0 collective-permute-done.6
  88.5 0.0 copy-done.1
  88.5 0.1 fusion
  88.6 1.2 copy.24
  89.8 7.3 %all-to-all-done.4 = bf16[16,8,512]{2,1,0:T(8,128)(2,1)S(1)} async-done(((bf16[16,8,512]{2,1,0:T(8,128)(2,1)}), bf16[16,8,512]{2,1,0:T(8,128)(2,1)S(1)}, u32[]{:S(2)}, u32[]{:S(2)}) %all-to-all-start.4) | async-done | bytes 131104 | tf_op jit(solution)/shard_map/all_to_all | solution.py:20
  97.1 6.4 %all-to-all-start.2 = ((bf16[512,4,128]{2,1,0:T(4,128)(2,1)}), bf16[512,4,128]{2,1,0:T(4,128)(2,1)S(1)}, u32[]{:S(2)}, u32[]{:S(2)}) async-start(bf16[512,4,128]{2,1,0:T(4,128)(2,1)} %copy.24), calls=%async_computation.2 | async-start | bytes 1048576 | tf_op jit(solution)/shard_map/all_to_all | solution.py:193
  103.5 0.1 reshape.37
  103.6 0.7 reduce_sum.22
  104.2 18.0 %all-to-all-done.2 = bf16[512,4,128]{2,1,0:T(4,128)(2,1)S(1)} async-done(((bf16[512,4,128]{2,1,0:T(4,128)(2,1)}), bf16[512,4,128]{2,1,0:T(4,128)(2,1)S(1)}, u32[]{:S(2)}, u32[]{:S(2)}) %all-to-all-start.2) | async-done | bytes 524320 | tf_op jit(solution)/shard_map/all_to_all | solution.py:193
  122.3 1.0 copy.25
  (10 shorter events, 0.2 us)
Async XLA Ops:
  18.4 7.1 %copy-start.2 = (f32[4,4,512]{2,1,0:T(4,128)S(1)}, f32[4,4,512]{2,1,0:T(4,128)}, u32[]{:S(2)}) copy-start(f32[4,4,512]{2,1,0:T(4,128)} %param.14) | copy-start | bytes 98308
  18.4 7.2 %copy-start.3 = (bf16[4,512,128]{2,1,0:T(8,128)(2,1)S(1)}, bf16[4,512,128]{2,1,0:T(8,128)(2,1)}, u32[]{:S(2)}) copy-start(bf16[4,512,128]{2,1,0:T(8,128)(2,1)} %q_ref.1) | copy-start | bytes 1572868
  18.4 7.6 %copy-start.4 = (bf16[4,512,128]{2,1,0:T(8,128)(2,1)S(1)}, bf16[4,512,128]{2,1,0:T(8,128)(2,1)}, u32[]{:S(2)}) copy-start(bf16[4,512,128]{2,1,0:T(8,128)(2,1)} %k_ref.1) | copy-start | bytes 1572868
  18.4 7.7 %copy-start.5 = (bf16[4,512,128]{2,1,0:T(8,128)(2,1)S(1)}, bf16[4,512,128]{2,1,0:T(8,128)(2,1)}, u32[]{:S(2)}) copy-start(bf16[4,512,128]{2,1,0:T(8,128)(2,1)} %v_ref.1) | copy-start | bytes 1572868
  18.4 8.1 %copy-start.6 = (bf16[4,512,128]{2,1,0:T(8,128)(2,1)S(1)}, bf16[4,512,128]{2,1,0:T(8,128)(2,1)}, u32[]{:S(2)}) copy-start(bf16[4,512,128]{2,1,0:T(8,128)(2,1)} %o_ref.1) | copy-start | bytes 1572868
  19.6 21.2 %all-to-all-start.1 = ((bf16[8,128,512]{2,1,0:T(8,128)(2,1)}), bf16[8,128,512]{2,1,0:T(8,128)(2,1)S(1)}, u32[]{:S(2)}, u32[]{:S(2)}) async-start(bf16[8,128,512]{2,1,0:T(8,128)(2,1)} %broadcast_in_dim.17), calls=%async_computation.1 | async-start | bytes 2097152 | tf_op jit(solution)/shard_map/all_to_all | solution.py:20
  25.5 1.2 collective-permute-start.5
  25.6 4.1 %collective-permute-start = (bf16[4,512,128]{2,1,0:T(8,128)(2,1)S(1)}, bf16[4,512,128]{2,1,0:T(8,128)(2,1)}, u32[]{:S(2)}, u32[]{:S(2)}) collective-permute-start(bf16[4,512,128]{2,1,0:T(8,128)(2,1)S(1)} %copy-done.3), channel_id=1, source_target_pairs={{0,2},{2,0},{1,3},{3,1},{4,6},{6,4},{5,7},{7,5},{8,10},{10,8},{9,1... | collective-permute-start | bytes 1572872 | tf_op jit(solution)/shard_map/ppermute | solution.py:24
  26.0 3.7 %collective-permute-start.1 = (bf16[4,512,128]{2,1,0:T(8,128)(2,1)S(1)}, bf16[4,512,128]{2,1,0:T(8,128)(2,1)}, u32[]{:S(2)}, u32[]{:S(2)}) collective-permute-start(bf16[4,512,128]{2,1,0:T(8,128)(2,1)S(1)} %copy-done.4), channel_id=1, source_target_pairs={{0,2},{2,0},{1,3},{3,1},{4,6},{6,4},{5,7},{7,5},{8,10},{10,8},{9,1... | collective-permute-start | bytes 1572872 | tf_op jit(solution)/shard_map/ppermute | solution.py:24
  26.1 3.6 %collective-permute-start.2 = (bf16[4,512,128]{2,1,0:T(8,128)(2,1)S(1)}, bf16[4,512,128]{2,1,0:T(8,128)(2,1)}, u32[]{:S(2)}, u32[]{:S(2)}) collective-permute-start(bf16[4,512,128]{2,1,0:T(8,128)(2,1)S(1)} %copy-done.5), channel_id=1, source_target_pairs={{0,2},{2,0},{1,3},{3,1},{4,6},{6,4},{5,7},{7,5},{8,10},{10,8},{9,1... | collective-permute-start | bytes 1572872 | tf_op jit(solution)/shard_map/ppermute | solution.py:24
  26.5 3.4 %collective-permute-start.3 = (bf16[4,512,128]{2,1,0:T(8,128)(2,1)S(1)}, bf16[4,512,128]{2,1,0:T(8,128)(2,1)}, u32[]{:S(2)}, u32[]{:S(2)}) collective-permute-start(bf16[4,512,128]{2,1,0:T(8,128)(2,1)S(1)} %copy-done.6), channel_id=1, source_target_pairs={{0,2},{2,0},{1,3},{3,1},{4,6},{6,4},{5,7},{7,5},{8,10},{10,8},{9,1... | collective-permute-start | bytes 1572872 | tf_op jit(solution)/shard_map/ppermute | solution.py:24
  26.7 4.0 %collective-permute-start.4 = (bf16[4,512,128]{2,1,0:T(8,128)(2,1)}, bf16[4,512,128]{2,1,0:T(8,128)(2,1)}, u32[]{:S(2)}, u32[]{:S(2)}) collective-permute-start(bf16[4,512,128]{2,1,0:T(8,128)(2,1)} %g_ref.1), channel_id=1, source_target_pairs={{0,2},{2,0},{1,3},{3,1},{4,6},{6,4},{5,7},{7,5},{8,10},{10,8},{9,1... | collective-permute-start | bytes 1572872 | tf_op jit(solution)/shard_map/ppermute | solution.py:24
  40.8 1.0 copy-start
  64.5 4.8 %copy-start.7 = (bf16[4,512,128]{2,1,0:T(8,128)(2,1)S(1)}, bf16[4,512,128]{2,1,0:T(8,128)(2,1)}, u32[]{:S(2)}) copy-start(bf16[4,512,128]{2,1,0:T(8,128)(2,1)} %get-tuple-element.8) | copy-start | bytes 1572868
  64.5 24.0 %copy-start.1 = (f32[4,512,128]{2,1,0:T(8,128)S(1)}, f32[4,512,128]{2,1,0:T(8,128)}, u32[]{:S(2)}) copy-start(f32[4,512,128]{2,1,0:T(8,128)} %get-tuple-element.7) | copy-start | bytes 3145732
  64.5 19.5 %all-to-all-start.3 = ((bf16[8,128,512]{2,1,0:T(8,128)(2,1)}), bf16[8,128,512]{2,1,0:T(8,128)(2,1)S(1)}, u32[]{:S(2)}, u32[]{:S(2)}) async-start(bf16[8,128,512]{2,1,0:T(8,128)(2,1)} %bitcast.19), calls=%async_computation.3 | async-start | bytes 2097152 | tf_op jit(solution)/shard_map/all_to_all | solution.py:20
  69.3 19.2 %collective-permute-start.6 = (bf16[4,512,128]{2,1,0:T(8,128)(2,1)S(1)}, bf16[4,512,128]{2,1,0:T(8,128)(2,1)S(1)}, u32[]{:S(2)}, u32[]{:S(2)}) collective-permute-start(bf16[4,512,128]{2,1,0:T(8,128)(2,1)S(1)} %copy-done.7), channel_id=1, source_target_pairs={{0,2},{2,0},{1,3},{3,1},{4,6},{6,4},{5,7},{7,5},{8,10},{10,8},{9,1... | collective-permute-start | bytes 1572872 | tf_op jit(solution)/shard_map/ppermute | solution.py:24
  85.0 12.1 %all-to-all-start.4 = ((bf16[16,8,512]{2,1,0:T(8,128)(2,1)}), bf16[16,8,512]{2,1,0:T(8,128)(2,1)S(1)}, u32[]{:S(2)}, u32[]{:S(2)}) async-start(bf16[16,8,512]{2,1,0:T(8,128)(2,1)} %reshape.36), calls=%async_computation.4 | async-start | bytes 262144 | tf_op jit(solution)/shard_map/all_to_all | solution.py:20
  97.1 25.2 %all-to-all-start.2 = ((bf16[512,4,128]{2,1,0:T(4,128)(2,1)}), bf16[512,4,128]{2,1,0:T(4,128)(2,1)S(1)}, u32[]{:S(2)}, u32[]{:S(2)}) async-start(bf16[512,4,128]{2,1,0:T(4,128)(2,1)} %copy.24), calls=%async_computation.2 | async-start | bytes 1048576 | tf_op jit(solution)/shard_map/all_to_all | solution.py:193
